TPU v7x, 8 devices: a whole 2x2x1 slice. The times are simulated.
8 devices in a mesh: dp: 1 (over z), a: 2 (over y), b: 4 (over x, core).
Axes of the slice: x: 2, y: 2, z: 1, core: 2. Of those that a mesh axis runs over, the one named last changes fastest.
Arguments:
- x: bfloat16 [2048, 8192], P('dp', ('a', 'b'))
- w_gate: bfloat16 [8192, 28672], P('a', 'b')
- w_up: bfloat16 [8192, 28672], P('a', 'b')
- w_down: bfloat16 [28672, 8192], P('b', 'a')
Outputs:
- output: bfloat16 [2048, 8192], P('dp', ('a', 'b'))
All inputs are finite; a program needn't handle non-finite values.
Results may differ from a plain program's by a relative error of at most 0.016.
Values are sent between devices in bfloat16 or wider.
A program may use at most 2 GiB of HBM per device.

v0:
```python
import jax
import jax.numpy as jnp


def solution(mesh):
    def step(x, w_gate, w_up, w_down):
        gate, up = jnp.dot(x, w_gate), jnp.dot(x, w_up)
        hidden = (jax.nn.silu(gate.astype(jnp.float32)) * up.astype(jnp.float32)).astype(jnp.bfloat16)
        return jnp.dot(hidden, w_down)

    return step
```

profile of v0, /device:TPU:0, one launch (start us, length us, event | category | flops | bytes accessed | tf_op | source)
XLA Modules:
  0.0 1930.2 jit_solution(13521160506088999014)
XLA Ops:
  6.5 0.0 all-gather.4.cloned.1.call-start
  6.5 0.7 all-gather.4.cloned.1.call-update
  7.3 0.0 all-reduce.7.cloned.1.call-start
  7.3 108.6 %all-gather.4.cloned.1.call-done = bf16[2048,4096]{1,0:T(8,128)(2,1)} async-done(((bf16[2048,1024]{1,0:T(8,128)(2,1)}), bf16[2048,4096]{1,0:T(8,128)(2,1)}) %all-gather.4.cloned.1.call-update) | async-done | bytes 16777232 | tf_op args[0]
  115.9 133.6 %fusion.9 = bf16[2048,7168]{1,0:T(8,128)(2,1)} fusion(bf16[2048,4096]{1,0:T(8,128)(2,1)} %all-gather.4.cloned.1.call-done, bf16[4096,7168]{1,0:T(8,128)(2,1)} %param.2), kind=kOutput, calls=%fused_computation.10 | convolution fusion | flops 120259084288 | bytes 104857600 | tf_op jit(solution)/dot_general | solution.py:7
  249.5 143.8 %fusion.8 = bf16[2048,7168]{1,0:T(8,128)(2,1)} fusion(bf16[2048,4096]{1,0:T(8,128)(2,1)} %all-gather.4.cloned.1.call-done, bf16[4096,7168]{1,0:T(8,128)(2,1)} %param.1), kind=kOutput, calls=%fused_computation.9 | convolution fusion | flops 120259084288 | bytes 104857600 | tf_op jit(solution)/dot_general | solution.py:7
  393.3 0.0 all-reduce.7.cloned.1.call-update
  393.3 0.0 reduce-scatter.4.cloned.1.call-start
  393.4 1271.3 %all-reduce.7.cloned.1.call-done = (bf16[2048,7168]{1,0:T(8,128)(2,1)}, bf16[2048,7168]{1,0:T(8,128)(2,1)}) async-done(((bf16[2048,7168]{1,0:T(8,128)(2,1)}, bf16[2048,7168]{1,0:T(8,128)(2,1)}), (bf16[2048,7168]{1,0:T(8,128)(2,1)}, bf16[2048,7168]{1,0:T(8,128)(2,1)})) %all-reduce.7.cloned.1.call-update) | async-done | bytes 58720272 | tf_op jit(solution)/dot_general | solution.py:7
  1664.6 139.4 %fusion.5 = bf16[2048,4096]{1,0:T(8,128)(2,1)} fusion(bf16[7168,4096]{1,0:T(8,128)(2,1)} %param.3, bf16[2048,7168]{1,0:T(8,128)(2,1)} %get-tuple-element.4, bf16[2048,7168]{1,0:T(8,128)(2,1)} %get-tuple-element.5), kind=kOutput, calls=%fused_computation.7 | convolution fusion | flops 120376524800 | bytes 134217728 | tf_op jit(solution)/dot_general | solution.py:9
  1804.0 0.0 reduce-scatter.4.cloned.1.call-update
  1804.0 119.3 %reduce-scatter.4.cloned.1.call-done = bf16[2048,1024]{1,0:T(8,128)(2,1)} async-done(((bf16[2048,4096]{1,0:T(8,128)(2,1)}), bf16[2048,1024]{1,0:T(8,128)(2,1)}) %reduce-scatter.4.cloned.1.call-update) | async-done | bytes 4194320
Async XLA Ops:
  6.5 109.4 %all-gather.4.cloned.1.call-start = ((), (), s32[]{:S(2)}) async-start(), calls=%async_computation.1 | async-start | bytes 20971520 | tf_op args[0]
  7.3 1657.4 %all-reduce.7.cloned.1.call-start = ((), (), s32[]{:S(2)}) async-start(), calls=%async_computation.3 | async-start | bytes 117440512 | tf_op jit(solution)/dot_general | solution.py:7
  393.3 1530.0 %reduce-scatter.4.cloned.1.call-start = ((), (), s32[]{:S(2)}) async-start(), calls=%async_computation.2 | async-start | bytes 20971520
Sparse Core Ops, SparseCore 0:
  8.9 107.0 all-gather.3
  393.4 1271.1 all-reduce.6
  1804.2 119.0 reduce-scatter.3
where the time goes:
time: 1940 us; the launch traced here: 1930 us
  waiting for transfers between devices  1500 us (77%)
  matrix products  417 us (21%)
    dot_general x1, waiting for transfers between devices, step(): gate, up = (jnp.dot(x, w_gate), jnp.dot(x, w_up))  1270 us
    dot_general x2, matrix products, step(): gate, up = (jnp.dot(x, w_gate), jnp.dot(x, w_up))  277 us
    unnamed x5, waiting for transfers between devices  229 us
    dot_general x1, matrix products, step(): return jnp.dot(hidden, w_down)  139 us
  transfers between devices with their start and end apart: 3, of which 3 were waited for; matrix products, arithmetic and copies ran while one was open for 0% of the time, Pallas kernels for 0%

commit v1 on v0

v1 whole, which is shorter than its diff:
```python
import jax
import jax.numpy as jnp
from jax import lax
from jax.experimental import pallas as pl
from jax.experimental.pallas import tpu as pltpu
from jax.sharding import PartitionSpec as P

MESH = pl.DeviceIdType.MESH
M = 128
TN = 512
SUB = 256


def _kernel(x_hbm, wg_hbm, wu_hbm, wd_hbm, y_hbm,
            xg, wring, stage, recv, hid, ystage, yrecv, yown, yout,
            wsem, xlsem, xssem, xrsem, pssem, prsem, hssem, hrsem, yssem, yrsem, yosem):
    f32, bf16 = jnp.float32, jnp.bfloat16
    rows, xcols = x_hbm.shape
    depth, ff = wg_hbm.shape
    dcols = wd_hbm.shape[1]
    half = ff // 2
    steps = rows // (2 * M)
    nt = ff // TN
    nd = dcols // TN
    per = xcols // TN

    dp = lax.axis_index("dp")
    a = lax.axis_index("a")
    b = lax.axis_index("b")
    chip, core = b // 2, b % 2
    peer = (dp, 1 - a, b)

    def mate(q):
        fx = 1 - q // 2
        fc = ((q + 1) // 2) % 2
        return 2 * (chip + fx - 2 * chip * fx) + core + fc - 2 * core * fc

    def w_copies(kind, i, slot):
        if kind == "gu":
            cols = pl.ds(pl.multiple_of(i * TN, TN), TN)
            return [pltpu.make_async_copy(w.at[:, cols], wring.at[slot, k], wsem.at[slot, k])
                    for k, w in enumerate((wg_hbm, wu_hbm))]
        cols = pl.ds(pl.multiple_of(mate(i // per) * xcols + (i % per) * TN, TN), TN)
        return [pltpu.make_async_copy(wd_hbm.at[pl.ds(k * half, half), cols],
                                      wring.at[slot, k, pl.ds(0, half)], wsem.at[slot, k])
                for k in range(2)]

    def w_start(kind, i, slot):
        for c in w_copies(kind, i, slot):
            c.start()

    def w_wait(kind, i, slot):
        for c in w_copies(kind, i, slot):
            c.wait()

    def x_rows(c):
        s, mine = c // 2, c % 2
        src = s * 2 * M + (a * mine + (1 - a) * (1 - mine)) * M
        return pl.ds(pl.multiple_of(src, M), M), pl.ds(pl.multiple_of(c * M, M), M)

    def x_local(c):
        src, dst = x_rows(c)
        return pltpu.make_async_copy(
            x_hbm.at[src], xg.at[dst, pl.ds(pl.multiple_of(b * xcols, xcols), xcols)], xlsem.at[c])

    def x_remote(c, q):
        src, dst = x_rows(c)
        return pltpu.make_async_remote_copy(
            src_ref=x_hbm.at[src], dst_ref=xg.at[dst, pl.ds(pl.multiple_of(b * xcols, xcols), xcols)],
            send_sem=xssem.at[c, q], recv_sem=xrsem.at[c, q],
            device_id=(dp, a, mate(q)), device_id_type=MESH)

    def x_wait(c):
        x_local(c).wait()
        for q in range(3):
            x_remote(c, q).wait_recv()

    def p_copy(t, n):
        return pltpu.make_async_remote_copy(
            src_ref=stage.at[n], dst_ref=recv.at[t % 2, n], send_sem=pssem.at[n], recv_sem=prsem.at[t % 2, n],
            device_id=peer, device_id_type=MESH)

    def h_copy(s, n, place):
        ref = hid.at[s % 3, pl.ds(pl.multiple_of(place * M, M), M), pl.ds(pl.multiple_of(n * TN, TN), TN)]
        return pltpu.make_async_remote_copy(
            src_ref=ref, dst_ref=ref, send_sem=hssem.at[s % 3, n], recv_sem=hrsem.at[s % 3, n],
            device_id=peer, device_id_type=MESH)

    def tiles(t, do_p, do_o, last_next):
        lo = 2 * M * t - (M if do_o else 0)
        size = M * (int(do_p) + int(do_o))
        xrow = pl.ds(lo if isinstance(lo, int) else pl.multiple_of(lo, M), size)
        if do_o:
            x_wait(2 * t - 1)
        if do_p:
            x_wait(2 * t)

        def tile(n, carry):
            slot = n % 2
            w_wait("gu", n, slot)

            @pl.when(n < nt - 1)
            def _():
                w_start("gu", n + 1, 1 - slot)

            @pl.when(n == nt - 1)
            def _():
                last_next()

            if do_o:
                p_copy(t - 1, n).wait()
            for j in range(TN // SUB):
                cols = pl.ds(j * SUB, SUB)
                xv = xg[xrow, :]
                g = jnp.dot(xv, wring[slot, 0, :, cols], preferred_element_type=f32)
                u = jnp.dot(xv, wring[slot, 1, :, cols], preferred_element_type=f32)
                if do_p:
                    stage[n, pl.ds(0, M), cols] = g[size - M:].astype(bf16)
                    stage[n, pl.ds(M, M), cols] = u[size - M:].astype(bf16)
                if do_o:
                    og = g[:M] + recv[(t - 1) % 2, n, pl.ds(0, M), cols].astype(f32)
                    ou = u[:M] + recv[(t - 1) % 2, n, pl.ds(M, M), cols].astype(f32)
                    h = og * jax.nn.sigmoid(og) * ou
                    hid[(t - 1) % 3, pl.ds(pl.multiple_of(a * M, M), M),
                        pl.ds(pl.multiple_of(n * TN + j * SUB, SUB), SUB)] = h.astype(bf16)
            if do_p:
                p_copy(t, n).start()
            if do_o:
                h_copy(t - 1, n, a).start()
            return carry

        lax.fori_loop(0, nt, tile, 0)

    def y_copy(s, q, h):
        cols = pl.ds(pl.multiple_of(h * TN, TN), TN)
        return pltpu.make_async_remote_copy(
            src_ref=ystage.at[q, :, cols], dst_ref=yrecv.at[s % 2, q, :, cols],
            send_sem=yssem.at[q, h], recv_sem=yrsem.at[s % 2, q, h],
            device_id=(dp, a, mate(q)), device_id_type=MESH)

    def y_out(s):
        return pltpu.make_async_copy(
            yout, y_hbm.at[pl.ds(pl.multiple_of(s * 2 * M, 2 * M), 2 * M)], yosem)

    def finish(s, first):
        for q in range(3):
            for h in range(per):
                y_copy(s, q, h).wait()
        if first is not True:
            @pl.when(jnp.logical_not(first))
            def _():
                y_out(s - 1).wait()

        def chunk(i, carry):
            r = pl.ds(pl.multiple_of(i * 32, 32), 32)
            acc = yown[r, :]
            for q in range(3):
                acc = acc + yrecv[s % 2, q, r, :].astype(f32)
            yout[r, :] = acc.astype(bf16)
            return carry

        lax.fori_loop(0, 2 * M // 32, chunk, 0)
        y_out(s).start()

    def down(s, last_next):
        def arrived(n, carry):
            h_copy(s, n, 1 - a).wait_recv()
            h_copy(s, n, a).wait_send()
            return carry

        lax.fori_loop(0, nt, arrived, 0)

        def tile(i, carry):
            slot = i % 2
            q, h = i // per, i % per
            w_wait("d", i, slot)

            @pl.when(i < nd - 1)
            def _():
                w_start("d", i + 1, 1 - slot)

            @pl.when(i == nd - 1)
            def _():
                last_next()

            for j in range(TN // SUB):
                wc = pl.ds(j * SUB, SUB)
                out = jnp.dot(hid[s % 3, :, pl.ds(0, half)], wring[slot, 0, pl.ds(0, half), wc],
                              preferred_element_type=f32)
                out = out + jnp.dot(hid[s % 3, :, pl.ds(half, half)], wring[slot, 1, pl.ds(0, half), wc],
                                    preferred_element_type=f32)
                cols = pl.ds(pl.multiple_of(h * TN + j * SUB, SUB), SUB)

                @pl.when(q < 3)
                def _():
                    ystage[q, :, cols] = out.astype(bf16)

                @pl.when(q == 3)
                def _():
                    yown[:, cols] = out

            @pl.when(q < 3)
            def _():
                y_copy(s, q, h).start()

            return carry

        lax.fori_loop(0, nd, tile, 0)

    w_start("gu", 0, 0)
    for c in range(2 * steps):
        x_local(c).start()

    barrier = pltpu.get_barrier_semaphore()
    pl.semaphore_signal(barrier, inc=1, device_id=peer, device_id_type=MESH)
    for q in range(3):
        pl.semaphore_signal(barrier, inc=1, device_id=(dp, a, mate(q)), device_id_type=MESH)
    pl.semaphore_wait(barrier, 4)

    def send_x(c, carry):
        for q in range(3):
            x_remote(c, q).start()
        return carry

    lax.fori_loop(0, 2 * steps, send_x, 0)

    gu0 = lambda: w_start("gu", 0, 0)
    d0 = lambda: w_start("d", 0, 0)

    tiles(0, True, False, gu0)
    tiles(1, True, True, gu0)
    tiles(2, True, True, d0)
    down(0, gu0)

    def step(t, carry):
        tiles(t, True, True, d0)
        finish(t - 3, t == 3)
        down(t - 2, gu0)
        return carry

    lax.fori_loop(3, steps, step, 0)

    tiles(steps, False, True, d0)
    finish(steps - 3, steps == 3)
    down(steps - 2, d0)
    finish(steps - 2, False)
    down(steps - 1, lambda: None)
    finish(steps - 1, False)
    y_out(steps - 1).wait()

    def drain(c, carry):
        for q in range(3):
            x_remote(c, q).wait_send()
        return carry

    lax.fori_loop(0, 2 * steps, drain, 0)


def solution(mesh):
    def body(x, wg, wu, wd):
        rows, xcols = x.shape
        depth, ff = wg.shape
        dcols = wd.shape[1]
        steps, nt, per = rows // (2 * M), ff // TN, xcols // TN
        bf16 = jnp.bfloat16
        anyspace = pl.BlockSpec(memory_space=pl.ANY)
        dma = pltpu.SemaphoreType.DMA
        return pl.pallas_call(
            _kernel,
            out_shape=jax.ShapeDtypeStruct(x.shape, x.dtype),
            in_specs=[anyspace] * 4,
            out_specs=anyspace,
            scratch_shapes=[
                pltpu.VMEM((rows, depth), bf16),
                pltpu.VMEM((2, 2, depth, TN), bf16),
                pltpu.VMEM((nt, 2 * M, TN), bf16),
                pltpu.VMEM((2, nt, 2 * M, TN), bf16),
                pltpu.VMEM((3, 2 * M, ff), bf16),
                pltpu.VMEM((3, 2 * M, xcols), bf16),
                pltpu.VMEM((2, 3, 2 * M, xcols), bf16),
                pltpu.VMEM((2 * M, xcols), jnp.float32),
                pltpu.VMEM((2 * M, xcols), bf16),
                dma((2, 2)),
                dma((2 * steps,)),
                dma((2 * steps, 3)),
                dma((2 * steps, 3)),
                dma((nt,)),
                dma((2, nt)),
                dma((3, nt)),
                dma((3, nt)),
                dma((3, per)),
                dma((2, 3, per)),
                dma(()),
            ],
            compiler_params=pltpu.CompilerParams(
                collective_id=0, has_side_effects=True, vmem_limit_bytes=67043328),
        )(x, wg, wu, wd)

    return jax.shard_map(
        body, mesh=mesh,
        in_specs=(P("dp", ("a", "b")), P("a", "b"), P("a", "b"), P("b", "a")),
        out_specs=P("dp", ("a", "b")), check_vma=False)
```

time: 1940 us -> 1000 us (0.52)
  waiting for transfers between devices: 1500 us -> 0 us
  Pallas kernels: 0 us -> 1000 us
  matrix products: 417 us -> 0 us
    dot_general x1 -> x0, waiting for transfers between devices: 1270 us -> none  [step(): gate, up = (jnp.dot(x, w_gate), jnp.dot(x, w_up))]
    pallas_call x0 -> x1, Pallas kernels: none -> 1000 us  [body(): pl.pallas_call(_kernel, out_shape=jax.ShapeDtypeStruct(x.shape, x.dtype),...]
    dot_general x3 -> x0, matrix products: 417 us -> none  [the longest x2 277 us: step(): gate, up = (jnp.dot(x, w_gate), jnp.dot(x, w_up))]
    unnamed x5 -> x0, waiting for transfers between devices: 229 us -> none
  transfers between devices with their start and end apart: 3 -> 0, of which waited for: 3 -> 0; matrix products, arithmetic and copies ran while one was open for 0% -> 0% of each run, Pallas kernels for 0% -> 0%
where the time goes in v1:
time: 1000 us
  Pallas kernels  1000 us (100%)
    pallas_call x1, Pallas kernels, body(): pl.pallas_call(_kernel, out_shape=jax.ShapeDtypeStruct(x.shape, x.dtype),...  1000 us

profile of v1, /device:TPU:0, one launch (start us, length us, event | category | flops | bytes accessed | tf_op | source)
XLA Modules:
  0.0 1004.8 jit_solution(6168339084424274298)
XLA Ops:
  0.0 1000.1 %shard_map.46 = bf16[2048,1024]{1,0:T(8,128)(2,1)} custom-call(bf16[2048,1024]{1,0:T(8,128)(2,1)} %x_hbm.1, bf16[4096,7168]{1,0:T(8,128)(2,1)} %wg_hbm.1, bf16[4096,7168]{1,0:T(8,128)(2,1)} %wu_hbm.1, bf16[7168,4096]{1,0:T(8,128)(2,1)} %wd_hbm.1), custom_call_target="tpu_custom_call" | custom-call | tf_op jit(solution)/shard_map/pallas_call | solution.py:268
  1000.1 4.6 copy.6

commit v2 on v1

v2 whole, which is shorter than its diff:
```python
import jax
import jax.numpy as jnp
from jax import lax
from jax.experimental import pallas as pl
from jax.experimental.pallas import tpu as pltpu
from jax.sharding import PartitionSpec as P

MESH = pl.DeviceIdType.MESH
M = 128
HM = M // 2
TN = 512
SUB = 512


def _kernel(x_hbm, wg_hbm, wu_hbm, wd_hbm, y_hbm,
            xg, wring, stage, recv, hid, ystage, yrecv, ymate, yown, yout, acc,
            wsem, xlsem, xssem, xrsem, x0ssem, x0rsem, pssem, prsem, p0ssem, p0rsem, hssem, hrsem,
            yssem, yrsem, ymsem, yosem):
    f32, bf16 = jnp.float32, jnp.bfloat16
    rows, xcols = x_hbm.shape
    depth, ff = wg_hbm.shape
    dcols = wd_hbm.shape[1]
    half = ff // 2
    steps = rows // (2 * M)
    nt = ff // TN
    nd = dcols // TN
    per = xcols // TN

    dp = lax.axis_index("dp")
    a = lax.axis_index("a")
    b = lax.axis_index("b")
    chip, core = b // 2, b % 2
    peer = (dp, 1 - a, b)

    def mate(q):
        fx = 1 - q // 2
        fc = ((q + 1) // 2) % 2
        return 2 * (chip + fx - 2 * chip * fx) + core + fc - 2 * core * fc

    def d_tile(o):
        late = o // 4
        return (1 - late) * (1 - o % 2) + late * (o // 2), (1 - late) * (o // 2) + late * (o % 2)

    def w_copies(kind, i, slot):
        if kind == "gu":
            cols = pl.ds(pl.multiple_of(i * TN, TN), TN)
            return [pltpu.make_async_copy(w.at[:, cols], wring.at[slot, k], wsem.at[slot, k])
                    for k, w in enumerate((wg_hbm, wu_hbm))]
        out = []
        for k in range(2):
            q, h = d_tile(i if kind == "d" else 2 * i + k)
            part = {"d": k, "d0": 0, "d1": 1}[kind]
            cols = pl.ds(pl.multiple_of(mate(q) * xcols + h * TN, TN), TN)
            out.append(pltpu.make_async_copy(wd_hbm.at[pl.ds(part * half, half), cols],
                                             wring.at[slot, k, pl.ds(0, half)], wsem.at[slot, k]))
        return out

    def w_start(kind, i, slot):
        for c in w_copies(kind, i, slot):
            c.start()

    def w_wait(kind, i, slot):
        for c in w_copies(kind, i, slot):
            c.wait()

    def x_rows(c):
        s, mine = c // 2, c % 2
        src = s * 2 * M + (a * mine + (1 - a) * (1 - mine)) * M
        return pl.ds(pl.multiple_of(src, M), M), pl.ds(pl.multiple_of(c * M, M), M)

    def x_local(c):
        src, dst = x_rows(c)
        return pltpu.make_async_copy(
            x_hbm.at[src], xg.at[dst, pl.ds(pl.multiple_of(b * xcols, xcols), xcols)], xlsem.at[c])

    def x_remote(c, q):
        src, dst = x_rows(c)
        return pltpu.make_async_remote_copy(
            src_ref=x_hbm.at[src], dst_ref=xg.at[dst, pl.ds(pl.multiple_of(b * xcols, xcols), xcols)],
            send_sem=xssem.at[c, q], recv_sem=xrsem.at[c, q],
            device_id=(dp, a, mate(q)), device_id_type=MESH)

    def x_wait(c):
        x_local(c).wait()
        for q in range(3):
            x_remote(c, q).wait_recv()

    def x_first(k, q):
        src = pl.ds(pl.multiple_of((1 - a) * M + k * HM, HM), HM)
        dst = pl.ds(k * HM, HM)
        if q < 2:
            cols = pl.ds(pl.multiple_of(b * xcols, xcols), xcols)
            source = x_hbm.at[src]
        else:
            cols = pl.ds(pl.multiple_of(mate(0) * xcols, xcols), xcols)
            source = xg.at[dst, cols]
        return pltpu.make_async_remote_copy(
            src_ref=source, dst_ref=xg.at[dst, cols], send_sem=x0ssem.at[q, k], recv_sem=x0rsem.at[q, k],
            device_id=(dp, a, mate(0 if q == 0 else 2)), device_id_type=MESH)

    def p_first(n, k):
        ref = pl.ds(k * M, M)
        return pltpu.make_async_remote_copy(
            src_ref=stage.at[n, ref], dst_ref=recv.at[0, n, ref], send_sem=p0ssem.at[n, k], recv_sem=p0rsem.at[n, k],
            device_id=peer, device_id_type=MESH)

    def first(last_next):
        def tile(n, carry):
            slot = n % 2
            w_wait("gu", n, slot)

            @pl.when(n < nt - 1)
            def _():
                w_start("gu", n + 1, 1 - slot)

            @pl.when(n == nt - 1)
            def _():
                last_next()

            for k in range(2):
                @pl.when(n == 0)
                def _():
                    if k == 0:
                        x_local(0).wait()
                    x_first(k, 0).wait_recv()
                    x_first(k, 2).start()
                    x_first(k, 1).wait_recv()
                    x_first(k, 2).wait_recv()

                for j in range(TN // SUB):
                    cols = pl.ds(j * SUB, SUB)
                    xv = xg[pl.ds(k * HM, HM), :]
                    g = jnp.dot(xv, wring[slot, 0, :, cols], preferred_element_type=f32)
                    u = jnp.dot(xv, wring[slot, 1, :, cols], preferred_element_type=f32)
                    stage[n, pl.ds(k * M, HM), cols] = g.astype(bf16)
                    stage[n, pl.ds(k * M + HM, HM), cols] = u.astype(bf16)
                p_first(n, k).start()

            for q in range(3):
                x_remote(n + 1, q).start()
            return carry

        lax.fori_loop(0, nt, tile, 0)
        for c in range(nt + 1, 2 * steps):
            for q in range(3):
                x_remote(c, q).start()

    def p_copy(t, n):
        return pltpu.make_async_remote_copy(
            src_ref=stage.at[n], dst_ref=recv.at[t % 2, n], send_sem=pssem.at[n], recv_sem=prsem.at[t % 2, n],
            device_id=peer, device_id_type=MESH)

    def h_copy(s, n, place):
        ref = hid.at[s % 3, pl.ds(pl.multiple_of(place * M, M), M), pl.ds(pl.multiple_of(n * TN, TN), TN)]
        return pltpu.make_async_remote_copy(
            src_ref=ref, dst_ref=ref, send_sem=hssem.at[s % 3, n], recv_sem=hrsem.at[s % 3, n],
            device_id=peer, device_id_type=MESH)

    def tiles(t, do_p, last_next):
        lo = 2 * M * t - M
        xrow = pl.ds(lo if isinstance(lo, int) else pl.multiple_of(lo, M), 2 * M if do_p else M)
        x_wait(2 * t - 1)
        if do_p:
            x_wait(2 * t)

        def tile(n, carry):
            slot = n % 2
            w_wait("gu", n, slot)

            @pl.when(n < nt - 1)
            def _():
                w_start("gu", n + 1, 1 - slot)

            @pl.when(n == nt - 1)
            def _():
                last_next()

            if isinstance(t, int) and t == 1:
                p_first(n, 0).wait()
                p_first(n, 1).wait()
            else:
                p_copy(t - 1, n).wait()
            for j in range(TN // SUB):
                cols = pl.ds(j * SUB, SUB)
                xv = xg[xrow, :]
                g = jnp.dot(xv, wring[slot, 0, :, cols], preferred_element_type=f32)
                u = jnp.dot(xv, wring[slot, 1, :, cols], preferred_element_type=f32)
                for k in range(2):
                    if do_p:
                        stage[n, pl.ds(k * M, HM), cols] = g[M + k * HM:M + (k + 1) * HM].astype(bf16)
                        stage[n, pl.ds(k * M + HM, HM), cols] = u[M + k * HM:M + (k + 1) * HM].astype(bf16)
                    og = g[k * HM:(k + 1) * HM] + recv[(t - 1) % 2, n, pl.ds(k * M, HM), cols].astype(f32)
                    ou = u[k * HM:(k + 1) * HM] + recv[(t - 1) % 2, n, pl.ds(k * M + HM, HM), cols].astype(f32)
                    h = og * jax.nn.sigmoid(og) * ou
                    hid[(t - 1) % 3, pl.ds(pl.multiple_of(a * M + k * HM, HM), HM),
                        pl.ds(pl.multiple_of(n * TN + j * SUB, SUB), SUB)] = h.astype(bf16)
            if do_p:
                p_copy(t, n).start()
            h_copy(t - 1, n, a).start()
            return carry

        lax.fori_loop(0, nt, tile, 0)

    def y_copy(s, q, h):
        cols = pl.ds(h * TN if isinstance(h, int) else pl.multiple_of(h * TN, TN), TN)
        dst = ymate.at[:, cols] if q == 1 else yrecv.at[s % 2, q // 2, :, cols]
        sem = ymsem.at[h] if q == 1 else yrsem.at[s % 2, q // 2, h]
        return pltpu.make_async_remote_copy(
            src_ref=ystage.at[q, :, cols], dst_ref=dst, send_sem=yssem.at[q, h], recv_sem=sem,
            device_id=(dp, a, mate(0 if q == 0 else 2)), device_id_type=MESH)

    def y_out(s, h):
        cols = pl.ds(h * TN, TN)
        return pltpu.make_async_copy(
            yout.at[:, cols], y_hbm.at[pl.ds(pl.multiple_of(s * 2 * M, 2 * M), 2 * M), cols], yosem.at[h])

    def finish(s, first):
        for h in range(per):
            for q in range(3):
                y_copy(s, q, h).wait_send()
            for q in (2, 0):
                y_copy(s, q, h).wait_recv()
            if first is not True:
                @pl.when(jnp.logical_not(first))
                def _():
                    y_out(s - 1, h).wait()

            def chunk(i, carry):
                r, cols = pl.ds(pl.multiple_of(i * 64, 64), 64), pl.ds(h * TN, TN)
                total = yown[r, cols] + yrecv[s % 2, 0, r, cols].astype(f32) + yrecv[s % 2, 1, r, cols].astype(f32)
                yout[r, cols] = total.astype(bf16)
                return carry

            lax.fori_loop(0, 2 * M // 64, chunk, 0)
            y_out(s, h).start()

    def arrived(s, lo, hi):
        def one(n, carry):
            h_copy(s, n, 1 - a).wait_recv()
            h_copy(s, n, a).wait_send()
            return carry

        lax.fori_loop(lo, hi, one, 0)

    def y_meet(q, h):
        @pl.when(q == 0)
        def _():
            y_copy(0, 1, h).wait_recv()

    def y_put(q, h, j, out):
        cols = pl.ds(pl.multiple_of(h * TN + j * SUB, SUB), SUB)

        @pl.when(q == 0)
        def _():
            ystage[0, :, cols] = (out + ymate[:, cols].astype(f32)).astype(bf16)

        @pl.when(jnp.logical_or(q == 1, q == 2))
        def _():
            ystage[q, :, cols] = out.astype(bf16)

        @pl.when(q == 3)
        def _():
            yown[:, cols] = out

    def y_send(s, q, h):
        for p in range(3):
            @pl.when(q == p)
            def _():
                y_copy(s, p, h).start()

    def down(s, last_next):
        arrived(s, 0, nt)

        def tile(i, carry):
            slot = i % 2
            q, h = d_tile(i)
            w_wait("d", i, slot)

            @pl.when(i < nd - 1)
            def _():
                w_start("d", i + 1, 1 - slot)

            @pl.when(i == nd - 1)
            def _():
                last_next()

            y_meet(q, h)
            for j in range(TN // SUB):
                wc = pl.ds(j * SUB, SUB)
                out = jnp.dot(hid[s % 3, :, pl.ds(0, half)], wring[slot, 0, pl.ds(0, half), wc],
                              preferred_element_type=f32)
                out = out + jnp.dot(hid[s % 3, :, pl.ds(half, half)], wring[slot, 1, pl.ds(0, half), wc],
                                    preferred_element_type=f32)
                y_put(q, h, j, out)
            y_send(s, q, h)
            return carry

        lax.fori_loop(0, nd, tile, 0)

    def down_last(s, p, between):
        arrived(s, p * (nt // 2), (p + 1) * (nt // 2))
        items = nd // 2

        def item(i, carry):
            slot = i % 2
            w_wait("d%d" % p, i, slot)

            @pl.when(i < items - 1)
            def _():
                w_start("d%d" % p, i + 1, 1 - slot)

            if p == 0:
                @pl.when(i == items - 1)
                def _():
                    w_start("d1", 0, 0)
                    between()

            for k in range(2):
                o = 2 * i + k
                q, h = d_tile(o)
                if p == 1:
                    y_meet(q, h)
                for j in range(TN // SUB):
                    wc = pl.ds(j * SUB, SUB)
                    out = jnp.dot(hid[s % 3, :, pl.ds(p * half, half)], wring[slot, k, pl.ds(0, half), wc],
                                  preferred_element_type=f32)
                    cols = pl.ds(k * TN + j * SUB, SUB)
                    if p == 0:
                        @pl.when(i < items - 1)
                        def _():
                            acc[i, :, cols] = out

                        @pl.when(i == items - 1)
                        def _():
                            yown[:, cols] = out
                    else:
                        @pl.when(i < items - 1)
                        def _():
                            y_put(q, h, j, acc[i, :, cols] + out)

                        @pl.when(i == items - 1)
                        def _():
                            yown[:, cols] = yown[:, cols] + out
                if p == 1:
                    y_send(s, q, h)
            return carry

        lax.fori_loop(0, items, item, 0)

    w_start("gu", 0, 0)
    for c in range(2 * steps):
        x_local(c).start()

    barrier = pltpu.get_barrier_semaphore()
    pl.semaphore_signal(barrier, inc=1, device_id=peer, device_id_type=MESH)
    for q in range(3):
        pl.semaphore_signal(barrier, inc=1, device_id=(dp, a, mate(q)), device_id_type=MESH)
    pl.semaphore_wait(barrier, 4)

    for q in range(2):
        for k in range(2):
            x_first(k, q).start()

    gu0 = lambda: w_start("gu", 0, 0)
    d0 = lambda: w_start("d", 0, 0)

    first(gu0)
    tiles(1, True, gu0)
    tiles(2, True, d0)
    down(0, gu0)

    def step(t, carry):
        tiles(t, True, d0)
        finish(t - 3, t == 3)
        down(t - 2, gu0)
        return carry

    lax.fori_loop(3, steps, step, 0)

    tiles(steps, False, d0)
    finish(steps - 3, steps == 3)
    down(steps - 2, lambda: w_start("d0", 0, 0))
    down_last(steps - 1, 0, lambda: finish(steps - 2, False))
    down_last(steps - 1, 1, None)
    finish(steps - 1, False)
    for h in range(per):
        y_out(steps - 1, h).wait()

    for k in range(2):
        for q in range(3):
            x_first(k, q).wait_send()

    def drain(c, carry):
        for q in range(3):
            x_remote(c, q).wait_send()
        return carry

    lax.fori_loop(1, 2 * steps, drain, 0)


def solution(mesh):
    def body(x, wg, wu, wd):
        rows, xcols = x.shape
        depth, ff = wg.shape
        dcols = wd.shape[1]
        steps, nt, per = rows // (2 * M), ff // TN, xcols // TN
        bf16 = jnp.bfloat16
        anyspace = pl.BlockSpec(memory_space=pl.ANY)
        dma = pltpu.SemaphoreType.DMA
        return pl.pallas_call(
            _kernel,
            out_shape=jax.ShapeDtypeStruct(x.shape, x.dtype),
            in_specs=[anyspace] * 4,
            out_specs=anyspace,
            scratch_shapes=[
                pltpu.VMEM((rows, depth), bf16),
                pltpu.VMEM((2, 2, depth, TN), bf16),
                pltpu.VMEM((nt, 2 * M, TN), bf16),
                pltpu.VMEM((2, nt, 2 * M, TN), bf16),
                pltpu.VMEM((3, 2 * M, ff), bf16),
                pltpu.VMEM((3, 2 * M, xcols), bf16),
                pltpu.VMEM((2, 2, 2 * M, xcols), bf16),
                pltpu.VMEM((2 * M, xcols), bf16),
                pltpu.VMEM((2 * M, xcols), jnp.float32),
                pltpu.VMEM((2 * M, xcols), bf16),
                pltpu.VMEM((dcols // (2 * TN) - 1, 2 * M, 2 * TN), jnp.float32),
                dma((2, 2)),
                dma((2 * steps,)),
                dma((2 * steps, 3)),
                dma((2 * steps, 3)),
                dma((3, 2)),
                dma((3, 2)),
                dma((nt,)),
                dma((2, nt)),
                dma((nt, 2)),
                dma((nt, 2)),
                dma((3, nt)),
                dma((3, nt)),
                dma((3, per)),
                dma((2, 2, per)),
                dma((per,)),
                dma((per,)),
            ],
            compiler_params=pltpu.CompilerParams(
                collective_id=0, has_side_effects=True, vmem_limit_bytes=67043328),
        )(x, wg, wu, wd)

    return jax.shard_map(
        body, mesh=mesh,
        in_specs=(P("dp", ("a", "b")), P("a", "b"), P("a", "b"), P("b", "a")),
        out_specs=P("dp", ("a", "b")), check_vma=False)
```

time: 1000 us -> 982 us (0.982)
  Pallas kernels: 1000 us -> 977 us
    pallas_call x1, Pallas kernels: 1000 us -> 977 us  [body(): pl.pallas_call(_kernel, out_shape=jax.ShapeDtypeStruct(x.shape, x.dtype),...]
where the time goes in v2:
time: 982 us
  Pallas kernels  977 us (99%)
    pallas_call x1, Pallas kernels, body(): pl.pallas_call(_kernel, out_shape=jax.ShapeDtypeStruct(x.shape, x.dtype),...  977 us

profile of v2, /device:TPU:0, one launch (start us, length us, event | category | flops | bytes accessed | tf_op | source)
XLA Modules:
  0.0 981.7 jit_solution(16419351418410473460)
XLA Ops:
  0.0 977.1 %shard_map.46 = bf16[2048,1024]{1,0:T(8,128)(2,1)} custom-call(bf16[2048,1024]{1,0:T(8,128)(2,1)} %x_hbm.1, bf16[4096,7168]{1,0:T(8,128)(2,1)} %wg_hbm.1, bf16[4096,7168]{1,0:T(8,128)(2,1)} %wu_hbm.1, bf16[7168,4096]{1,0:T(8,128)(2,1)} %wd_hbm.1), custom_call_target="tpu_custom_call" | custom-call | tf_op jit(solution)/shard_map/pallas_call | solution.py:410
  977.1 4.6 copy.6

commit v3 on v2

v3 whole, which is shorter than its diff:
```python
import jax
import jax.numpy as jnp
from jax import lax
from jax.experimental import pallas as pl
from jax.experimental.pallas import tpu as pltpu
from jax.sharding import PartitionSpec as P

MESH = pl.DeviceIdType.MESH
M = 128
HM = M // 2
TN = 512
SUB = 512


def _kernel(x_hbm, wg_hbm, wu_hbm, wd_hbm, y_hbm,
            xg, wring, stage, recv, hid, ystage, yrecv, ymate, yown, yout, acc,
            wsem, xlsem, xssem, xrsem, x0ssem, x0rsem, pssem, prsem, p0ssem, p0rsem, hssem, hrsem, hlssem, hlrsem,
            yssem, yrsem, ymsem, yosem, ylssem, ylrsem, ylmsem, ylosem):
    f32, bf16 = jnp.float32, jnp.bfloat16
    rows, xcols = x_hbm.shape
    depth, ff = wg_hbm.shape
    dcols = wd_hbm.shape[1]
    half = ff // 2
    steps = rows // (2 * M)
    nt = ff // TN
    nd = dcols // TN
    per = xcols // TN

    dp = lax.axis_index("dp")
    a = lax.axis_index("a")
    b = lax.axis_index("b")
    chip, core = b // 2, b % 2
    peer = (dp, 1 - a, b)

    def mate(q):
        fx = 1 - q // 2
        fc = ((q + 1) // 2) % 2
        return 2 * (chip + fx - 2 * chip * fx) + core + fc - 2 * core * fc

    def d_tile(o):
        late = o // 4
        return (1 - late) * (1 - o % 2) + late * (o // 2), (1 - late) * (o // 2) + late * (o % 2)

    def w_copy(kind, i, slot, k):
        if kind == "gu":
            cols = pl.ds(pl.multiple_of(i * TN, TN), TN)
            return pltpu.make_async_copy((wg_hbm, wu_hbm)[k].at[:, cols], wring.at[slot, k], wsem.at[slot, k])
        q, h = d_tile(i if kind == "d" else 2 * i + k)
        part = {"d": k, "d0": 0, "d1": 1}[kind]
        cols = pl.ds(pl.multiple_of(mate(q) * xcols + h * TN, TN), TN)
        return pltpu.make_async_copy(
            wd_hbm.at[pl.ds(part * half, half), cols], wring.at[slot, k, pl.ds(0, half)], wsem.at[slot, k])

    def w_wait(kind, i, slot, k):
        w_copy(kind, i, slot, k).wait()

    def w_ahead(kind, i, count, then, slot, k):
        @pl.when(i < count - 2)
        def _():
            w_copy(kind, i + 2, slot, k).start()

        if then is not None:
            @pl.when(i >= count - 2)
            def _():
                w_copy(then, i + 2 - count, slot, k).start()

    def x_rows(c):
        s, mine = c // 2, c % 2
        src = s * 2 * M + (a * mine + (1 - a) * (1 - mine)) * M
        return pl.ds(pl.multiple_of(src, M), M), pl.ds(pl.multiple_of(c * M, M), M)

    def x_local(c):
        src, dst = x_rows(c)
        return pltpu.make_async_copy(
            x_hbm.at[src], xg.at[dst, pl.ds(pl.multiple_of(b * xcols, xcols), xcols)], xlsem.at[c])

    def x_remote(c, q):
        src, dst = x_rows(c)
        return pltpu.make_async_remote_copy(
            src_ref=x_hbm.at[src], dst_ref=xg.at[dst, pl.ds(pl.multiple_of(b * xcols, xcols), xcols)],
            send_sem=xssem.at[c, q], recv_sem=xrsem.at[c, q],
            device_id=(dp, a, mate(q)), device_id_type=MESH)

    def x_wait(c):
        x_local(c).wait()
        for q in range(3):
            x_remote(c, q).wait_recv()

    def x_first(k, q):
        src = pl.ds(pl.multiple_of((1 - a) * M + k * HM, HM), HM)
        dst = pl.ds(k * HM, HM)
        if q < 2:
            cols = pl.ds(pl.multiple_of(b * xcols, xcols), xcols)
            source = x_hbm.at[src]
        else:
            cols = pl.ds(pl.multiple_of(mate(0) * xcols, xcols), xcols)
            source = xg.at[dst, cols]
        return pltpu.make_async_remote_copy(
            src_ref=source, dst_ref=xg.at[dst, cols], send_sem=x0ssem.at[q, k], recv_sem=x0rsem.at[q, k],
            device_id=(dp, a, mate(0 if q == 0 else 2)), device_id_type=MESH)

    def p_first(n, k, z):
        ref = pl.ds(k * M + z * HM, HM)
        return pltpu.make_async_remote_copy(
            src_ref=stage.at[n, ref], dst_ref=recv.at[0, n, ref], send_sem=p0ssem.at[n, 2 * k + z],
            recv_sem=p0rsem.at[n, 2 * k + z], device_id=peer, device_id_type=MESH)

    def first(then):
        def tile(n, carry):
            slot = n % 2
            for k in range(2):
                @pl.when(n == 0)
                def _():
                    if k == 0:
                        x_local(0).wait()
                    x_first(k, 0).wait_recv()
                    x_first(k, 2).start()
                    x_first(k, 1).wait_recv()
                    x_first(k, 2).wait_recv()

                for z in range(2):
                    if k == 0:
                        w_wait("gu", n, slot, z)
                    for j in range(TN // SUB):
                        cols = pl.ds(j * SUB, SUB)
                        out = jnp.dot(xg[pl.ds(k * HM, HM), :], wring[slot, z, :, cols], preferred_element_type=f32)
                        stage[n, pl.ds(k * M + z * HM, HM), cols] = out.astype(bf16)
                    p_first(n, k, z).start()
                    if k == 1:
                        w_ahead("gu", n, nt, then, slot, z)

            for q in range(3):
                x_remote(n + 1, q).start()
            return carry

        lax.fori_loop(0, nt, tile, 0)
        for c in range(nt + 1, 2 * steps):
            for q in range(3):
                x_remote(c, q).start()

    def p_copy(t, n):
        return pltpu.make_async_remote_copy(
            src_ref=stage.at[n], dst_ref=recv.at[t % 2, n], send_sem=pssem.at[n], recv_sem=prsem.at[t % 2, n],
            device_id=peer, device_id_type=MESH)

    def h_copy(s, n, place):
        ref = hid.at[s % 3, pl.ds(pl.multiple_of(place * M, M), M), pl.ds(pl.multiple_of(n * TN, TN), TN)]
        return pltpu.make_async_remote_copy(
            src_ref=ref, dst_ref=ref, send_sem=hssem.at[s % 3, n], recv_sem=hrsem.at[s % 3, n],
            device_id=peer, device_id_type=MESH)

    def h_half(s, n, k, place):
        ref = hid.at[s % 3, pl.ds(pl.multiple_of(k * M + place * HM, HM), HM), pl.ds(pl.multiple_of(n * TN, TN), TN)]
        return pltpu.make_async_remote_copy(
            src_ref=ref, dst_ref=ref, send_sem=hlssem.at[n, k], recv_sem=hlrsem.at[n, k],
            device_id=peer, device_id_type=MESH)

    def tiles(t, do_p, then, p_late=False):
        lo = 2 * M * t - M
        xrow = pl.ds(lo if isinstance(lo, int) else pl.multiple_of(lo, M), 2 * M if do_p else M)
        x_wait(2 * t - 1)
        if do_p:
            x_wait(2 * t)

        def tile(n, carry):
            slot = n % 2
            if isinstance(t, int) and t == 1:
                for k in range(2):
                    for z in range(2):
                        p_first(n, k, z).wait()
            else:
                p_copy(t - 1, n).wait()
            for j in range(TN // SUB):
                cols = pl.ds(j * SUB, SUB)
                xv = xg[xrow, :]
                w_wait("gu", n, slot, 0)
                g = jnp.dot(xv, wring[slot, 0, :, cols], preferred_element_type=f32)
                w_ahead("gu", n, nt, then, slot, 0)
                w_wait("gu", n, slot, 1)
                u = jnp.dot(xv, wring[slot, 1, :, cols], preferred_element_type=f32)
                w_ahead("gu", n, nt, then, slot, 1)
                for k in range(2):
                    if do_p:
                        stage[n, pl.ds(k * M, HM), cols] = g[M + k * HM:M + (k + 1) * HM].astype(bf16)
                        stage[n, pl.ds(k * M + HM, HM), cols] = u[M + k * HM:M + (k + 1) * HM].astype(bf16)
                    og = g[k * HM:(k + 1) * HM] + recv[(t - 1) % 2, n, pl.ds(k * M, HM), cols].astype(f32)
                    ou = u[k * HM:(k + 1) * HM] + recv[(t - 1) % 2, n, pl.ds(k * M + HM, HM), cols].astype(f32)
                    h = og * jax.nn.sigmoid(og) * ou
                    hrow = a * M + k * HM if do_p else k * M + a * HM
                    hid[(t - 1) % 3, pl.ds(pl.multiple_of(hrow, HM), HM),
                        pl.ds(pl.multiple_of(n * TN + j * SUB, SUB), SUB)] = h.astype(bf16)
            if do_p and not p_late:
                p_copy(t, n).start()
            if do_p:
                h_copy(t - 1, n, a).start()
            else:
                h_half(t - 1, n, 0, a).start()
            return carry

        lax.fori_loop(0, nt, tile, 0)

        def after(n, carry):
            if do_p:
                p_copy(t, n).start()
            else:
                h_half(t - 1, n, 1, a).start()
            return carry

        if p_late or not do_p:
            lax.fori_loop(0, nt, after, 0)

    def y_copy(s, q, h, k=None):
        cols = pl.ds(h * TN if isinstance(h, int) else pl.multiple_of(h * TN, TN), TN)
        r = pl.ds(0, 2 * M) if k is None else pl.ds(k * M, M)
        dst = ymate.at[r, cols] if q == 1 else yrecv.at[s % 2, q // 2, r, cols]
        if k is None:
            send, sem = yssem.at[q, h], ymsem.at[h] if q == 1 else yrsem.at[s % 2, q // 2, h]
        else:
            send, sem = ylssem.at[q, h, k], ylmsem.at[h, k] if q == 1 else ylrsem.at[q // 2, h, k]
        return pltpu.make_async_remote_copy(
            src_ref=ystage.at[q, r, cols], dst_ref=dst, send_sem=send, recv_sem=sem,
            device_id=(dp, a, mate(0 if q == 0 else 2)), device_id_type=MESH)

    def y_out(s, h):
        cols = pl.ds(h * TN, TN)
        return pltpu.make_async_copy(
            yout.at[:, cols], y_hbm.at[pl.ds(pl.multiple_of(s * 2 * M, 2 * M), 2 * M), cols], yosem.at[h])

    def finish(s, first):
        for h in range(per):
            for q in range(3):
                y_copy(s, q, h).wait_send()
            for q in (2, 0):
                y_copy(s, q, h).wait_recv()
            if first is not True:
                @pl.when(jnp.logical_not(first))
                def _():
                    y_out(s - 1, h).wait()

            def chunk(i, carry):
                r, cols = pl.ds(pl.multiple_of(i * 64, 64), 64), pl.ds(h * TN, TN)
                total = yown[r, cols] + yrecv[s % 2, 0, r, cols].astype(f32) + yrecv[s % 2, 1, r, cols].astype(f32)
                yout[r, cols] = total.astype(bf16)
                return carry

            lax.fori_loop(0, 2 * M // 64, chunk, 0)
            y_out(s, h).start()

    def arrived(s, lo, hi):
        def one(n, carry):
            h_copy(s, n, 1 - a).wait_recv()
            h_copy(s, n, a).wait_send()
            return carry

        lax.fori_loop(lo, hi, one, 0)

    def y_meet(q, h, k=None):
        @pl.when(q == 0)
        def _():
            y_copy(0, 1, h, k).wait_recv()

    def y_put(q, h, j, out, k=None):
        cols = pl.ds(pl.multiple_of(h * TN + j * SUB, SUB), SUB)
        r = pl.ds(0, 2 * M) if k is None else pl.ds(k * M, M)

        @pl.when(q == 0)
        def _():
            ystage[0, r, cols] = (out + ymate[r, cols].astype(f32)).astype(bf16)

        @pl.when(jnp.logical_or(q == 1, q == 2))
        def _():
            ystage[q, r, cols] = out.astype(bf16)

        @pl.when(q == 3)
        def _():
            yown[r, cols] = out

    def y_send(s, q, h, k=None):
        for p in range(3):
            @pl.when(q == p)
            def _():
                y_copy(s, p, h, k).start()

    def down(s, then):
        arrived(s, 0, nt)

        def tile(i, carry):
            slot = i % 2
            q, h = d_tile(i)
            y_meet(q, h)
            w_wait("d", i, slot, 0)
            w_wait("d", i, slot, 1)
            out = jnp.dot(hid[s % 3, :, pl.ds(0, half)], wring[slot, 0, pl.ds(0, half)],
                          preferred_element_type=f32)
            out = out + jnp.dot(hid[s % 3, :, pl.ds(half, half)], wring[slot, 1, pl.ds(0, half)],
                                preferred_element_type=f32)
            y_put(q, h, 0, out)
            w_ahead("d", i, nd, then, slot, 0)
            w_ahead("d", i, nd, then, slot, 1)
            y_send(s, q, h)
            return carry

        lax.fori_loop(0, nd, tile, 0)

    def y_out_last(s, k, h, place):
        cols = pl.ds(h * TN, TN)
        return pltpu.make_async_copy(
            yout.at[pl.ds(k * M + place * HM, HM), cols],
            y_hbm.at[pl.ds(s * 2 * M + place * M + k * HM, HM), cols], ylosem.at[k, h, place])

    def finish_last(s, k):
        for h in range(per):
            for q in range(3):
                y_copy(s, q, h, k).wait_send()
            for q in (2, 0):
                y_copy(s, q, h, k).wait_recv()
            if k == 0:
                y_out(s - 1, h).wait()
            r, cols = pl.ds(k * M, M), pl.ds(h * TN, TN)
            total = yown[r, cols] + yrecv[s % 2, 0, r, cols].astype(f32) + yrecv[s % 2, 1, r, cols].astype(f32)
            yout[r, cols] = total.astype(bf16)
            for place in range(2):
                y_out_last(s, k, h, place).start()

    def down_last(s, k, p, then):
        def one(n, carry):
            h_half(s, n, k, 1 - a).wait_recv()
            h_half(s, n, k, a).wait_send()
            return carry

        lax.fori_loop(p * (nt // 2), (p + 1) * (nt // 2), one, 0)
        items = nd // 2

        def item(i, carry):
            slot = i % 2
            r = pl.ds(k * M, M)
            for e in range(2):
                q, h = d_tile(2 * i + e)
                if p == 1:
                    y_meet(q, h, k)
                w_wait("d%d" % p, i, slot, e)
                for j in range(TN // SUB):
                    wc = pl.ds(j * SUB, SUB)
                    out = jnp.dot(hid[s % 3, r, pl.ds(p * half, half)], wring[slot, e, pl.ds(0, half), wc],
                                  preferred_element_type=f32)
                    cols = pl.ds(e * TN + j * SUB, SUB)
                    if p == 0:
                        acc[i, :, cols] = out
                    else:
                        y_put(q, h, j, acc[i, :, cols] + out, k)
                w_ahead("d%d" % p, i, items, then, slot, e)
                if p == 1:
                    y_send(s, q, h, k)
            return carry

        lax.fori_loop(0, items, item, 0)

    for i in range(2):
        for k in range(2):
            w_copy("gu", i, i, k).start()
    for c in range(2 * steps):
        x_local(c).start()

    barrier = pltpu.get_barrier_semaphore()
    pl.semaphore_signal(barrier, inc=1, device_id=peer, device_id_type=MESH)
    for q in range(3):
        pl.semaphore_signal(barrier, inc=1, device_id=(dp, a, mate(q)), device_id_type=MESH)
    pl.semaphore_wait(barrier, 4)

    for q in range(2):
        for k in range(2):
            x_first(k, q).start()

    first("gu")
    tiles(1, True, "gu")
    tiles(2, True, "d")
    down(0, "gu")

    def step(t, carry):
        tiles(t, True, "d")
        finish(t - 3, t == 3)
        down(t - 2, "gu")
        return carry

    last = steps - 1
    lax.fori_loop(3, last, step, 0)

    tiles(last, True, "d", p_late=True)
    finish(last - 3, False)
    down(last - 2, "d")
    finish(last - 2, False)
    down(last - 1, "gu")
    tiles(steps, False, "d0")
    finish(last - 1, False)
    down_last(last, 0, 0, "d1")
    down_last(last, 0, 1, "d0")
    down_last(last, 1, 0, "d1")
    finish_last(last, 0)
    down_last(last, 1, 1, None)
    finish_last(last, 1)
    for k in range(2):
        for h in range(per):
            for place in range(2):
                y_out_last(last, k, h, place).wait()

    for k in range(2):
        for q in range(3):
            x_first(k, q).wait_send()

    def drain(c, carry):
        for q in range(3):
            x_remote(c, q).wait_send()
        return carry

    lax.fori_loop(1, 2 * steps, drain, 0)


def solution(mesh):
    def body(x, wg, wu, wd):
        rows, xcols = x.shape
        depth, ff = wg.shape
        dcols = wd.shape[1]
        steps, nt, per = rows // (2 * M), ff // TN, xcols // TN
        bf16 = jnp.bfloat16
        anyspace = pl.BlockSpec(memory_space=pl.ANY)
        dma = pltpu.SemaphoreType.DMA
        return pl.pallas_call(
            _kernel,
            out_shape=jax.ShapeDtypeStruct(x.shape, x.dtype),
            in_specs=[anyspace] * 4,
            out_specs=anyspace,
            scratch_shapes=[
                pltpu.VMEM((rows, depth), bf16),
                pltpu.VMEM((2, 2, depth, TN), bf16),
                pltpu.VMEM((nt, 2 * M, TN), bf16),
                pltpu.VMEM((2, nt, 2 * M, TN), bf16),
                pltpu.VMEM((3, 2 * M, ff), bf16),
                pltpu.VMEM((3, 2 * M, xcols), bf16),
                pltpu.VMEM((2, 2, 2 * M, xcols), bf16),
                pltpu.VMEM((2 * M, xcols), bf16),
                pltpu.VMEM((2 * M, xcols), jnp.float32),
                pltpu.VMEM((2 * M, xcols), bf16),
                pltpu.VMEM((dcols // (2 * TN), M, 2 * TN), jnp.float32),
                dma((2, 2)),
                dma((2 * steps,)),
                dma((2 * steps, 3)),
                dma((2 * steps, 3)),
                dma((3, 2)),
                dma((3, 2)),
                dma((nt,)),
                dma((2, nt)),
                dma((nt, 4)),
                dma((nt, 4)),
                dma((3, nt)),
                dma((3, nt)),
                dma((nt, 2)),
                dma((nt, 2)),
                dma((3, per)),
                dma((2, 2, per)),
                dma((per,)),
                dma((per,)),
                dma((3, per, 2)),
                dma((2, per, 2)),
                dma((per, 2)),
                dma((2, per, 2)),
            ],
            compiler_params=pltpu.CompilerParams(
                collective_id=0, has_side_effects=True, vmem_limit_bytes=67043328),
        )(x, wg, wu, wd)

    return jax.shard_map(
        body, mesh=mesh,
        in_specs=(P("dp", ("a", "b")), P("a", "b"), P("a", "b"), P("b", "a")),
        out_specs=P("dp", ("a", "b")), check_vma=False)
```

time: 982 us -> 976 us (level)
  no operation moved by 1% of the time
where the time goes in v3:
time: 976 us
  Pallas kernels  971 us (99%)
    pallas_call x1, Pallas kernels, body(): pl.pallas_call(_kernel, out_shape=jax.ShapeDtypeStruct(x.shape, x.dtype),...  971 us

profile of v3, /device:TPU:0, one launch (start us, length us, event | category | flops | bytes accessed | tf_op | source)
XLA Modules:
  0.0 976.1 jit_solution(7906653301551661710)
XLA Ops:
  0.0 971.4 %shard_map.46 = bf16[2048,1024]{1,0:T(8,128)(2,1)} custom-call(bf16[2048,1024]{1,0:T(8,128)(2,1)} %x_hbm.1, bf16[4096,7168]{1,0:T(8,128)(2,1)} %wg_hbm.1, bf16[4096,7168]{1,0:T(8,128)(2,1)} %wu_hbm.1, bf16[7168,4096]{1,0:T(8,128)(2,1)} %wd_hbm.1), custom_call_target="tpu_custom_call" | custom-call | tf_op jit(solution)/shard_map/pallas_call | solution.py:427
  971.4 4.6 copy.6

commit v4 on v3

--- a/solution.py
+++ b/solution.py
@@ -138,15 +138,16 @@
             for q in range(3):
                 x_remote(c, q).start()
 
-    def p_copy(t, n):
-        return pltpu.make_async_remote_copy(
-            src_ref=stage.at[n], dst_ref=recv.at[t % 2, n], send_sem=pssem.at[n], recv_sem=prsem.at[t % 2, n],
+    def p_copy(t, m):
+        pair = pl.ds(2 * m, 2)
+        return pltpu.make_async_remote_copy(
+            src_ref=stage.at[pair], dst_ref=recv.at[t % 2, pair], send_sem=pssem.at[m], recv_sem=prsem.at[t % 2, m],
             device_id=peer, device_id_type=MESH)
 
-    def h_copy(s, n, place):
-        ref = hid.at[s % 3, pl.ds(pl.multiple_of(place * M, M), M), pl.ds(pl.multiple_of(n * TN, TN), TN)]
-        return pltpu.make_async_remote_copy(
-            src_ref=ref, dst_ref=ref, send_sem=hssem.at[s % 3, n], recv_sem=hrsem.at[s % 3, n],
+    def h_copy(s, m, place):
+        ref = hid.at[s % 3, pl.ds(pl.multiple_of(place * M, M), M), pl.ds(pl.multiple_of(m * 2 * TN, 2 * TN), 2 * TN)]
+        return pltpu.make_async_remote_copy(
+            src_ref=ref, dst_ref=ref, send_sem=hssem.at[s % 3, m], recv_sem=hrsem.at[s % 3, m],
             device_id=peer, device_id_type=MESH)
 
     def h_half(s, n, k, place):
@@ -169,7 +170,9 @@
                     for z in range(2):
                         p_first(n, k, z).wait()
             else:
-                p_copy(t - 1, n).wait()
+                @pl.when(n % 2 == 0)
+                def _():
+                    p_copy(t - 1, n // 2).wait()
             for j in range(TN // SUB):
                 cols = pl.ds(j * SUB, SUB)
                 xv = xg[xrow, :]
@@ -189,10 +192,12 @@
                     hrow = a * M + k * HM if do_p else k * M + a * HM
                     hid[(t - 1) % 3, pl.ds(pl.multiple_of(hrow, HM), HM),
                         pl.ds(pl.multiple_of(n * TN + j * SUB, SUB), SUB)] = h.astype(bf16)
-            if do_p and not p_late:
-                p_copy(t, n).start()
             if do_p:
-                h_copy(t - 1, n, a).start()
+                @pl.when(n % 2 == 1)
+                def _():
+                    if not p_late:
+                        p_copy(t, n // 2).start()
+                    h_copy(t - 1, n // 2, a).start()
             else:
                 h_half(t - 1, n, 0, a).start()
             return carry
@@ -207,7 +212,7 @@
             return carry
 
         if p_late or not do_p:
-            lax.fori_loop(0, nt, after, 0)
+            lax.fori_loop(0, nt // 2 if do_p else nt, after, 0)
 
     def y_copy(s, q, h, k=None):
         cols = pl.ds(h * TN if isinstance(h, int) else pl.multiple_of(h * TN, TN), TN)
@@ -246,13 +251,13 @@
             lax.fori_loop(0, 2 * M // 64, chunk, 0)
             y_out(s, h).start()
 
-    def arrived(s, lo, hi):
-        def one(n, carry):
-            h_copy(s, n, 1 - a).wait_recv()
-            h_copy(s, n, a).wait_send()
-            return carry
-
-        lax.fori_loop(lo, hi, one, 0)
+    def arrived(s):
+        def one(m, carry):
+            h_copy(s, m, 1 - a).wait_recv()
+            h_copy(s, m, a).wait_send()
+            return carry
+
+        lax.fori_loop(0, nt // 2, one, 0)
 
     def y_meet(q, h, k=None):
         @pl.when(q == 0)
@@ -282,7 +287,7 @@
                 y_copy(s, p, h, k).start()
 
     def down(s, then):
-        arrived(s, 0, nt)
+        arrived(s)
 
         def tile(i, carry):
             slot = i % 2
@@ -447,12 +452,12 @@
                 dma((2 * steps, 3)),
                 dma((3, 2)),
                 dma((3, 2)),
-                dma((nt,)),
-                dma((2, nt)),
+                dma((nt // 2,)),
+                dma((2, nt // 2)),
                 dma((nt, 4)),
                 dma((nt, 4)),
-                dma((3, nt)),
-                dma((3, nt)),
+                dma((3, nt // 2)),
+                dma((3, nt // 2)),
                 dma((nt, 2)),
                 dma((nt, 2)),
                 dma((3, per)),

time: 976 us -> 976 us (level)
  no operation moved by 1% of the time
where the time goes in v4:
time: 976 us; the launch traced here: 975 us
  Pallas kernels  971 us (99%)
    pallas_call x1, Pallas kernels, body(): pl.pallas_call(_kernel, out_shape=jax.ShapeDtypeStruct(x.shape, x.dtype),...  971 us

profile of v4, /device:TPU:0, one launch (start us, length us, event | category | flops | bytes accessed | tf_op | source)
XLA Modules:
  0.0 975.5 jit_solution(6547698624141418958)
XLA Ops:
  0.0 970.8 %shard_map.46 = bf16[2048,1024]{1,0:T(8,128)(2,1)} custom-call(bf16[2048,1024]{1,0:T(8,128)(2,1)} %x_hbm.1, bf16[4096,7168]{1,0:T(8,128)(2,1)} %wg_hbm.1, bf16[4096,7168]{1,0:T(8,128)(2,1)} %wu_hbm.1, bf16[7168,4096]{1,0:T(8,128)(2,1)} %wd_hbm.1), custom_call_target="tpu_custom_call" | custom-call | tf_op jit(solution)/shard_map/pallas_call | solution.py:432
  970.9 4.6 copy.6
